TPU v7x, 256 devices: a whole 4x4x8 slice. The times are simulated.
256 devices in a mesh: tp: 16 (over z_lo, y), dp: 16 (over z_hi, x, core).
Axes of the slice: x: 4, y: 4, z: 8 (z_hi: 2, z_lo: 4; z = z_hi * 4 + z_lo), core: 2. Of those that a mesh axis runs over, the one named last changes fastest.
Arguments:
- normed: bfloat16 [8192, 4096], P(('dp', 'tp')), may hold values from -6 to 6
- cotangent: bfloat16 [8192, 8192], P('dp', 'tp'), may hold values from -0.52734375 to 0.52734375
- weight_tiles: bfloat16 [2, 2048, 128, 128], P(None, 'tp'), may hold values from -0.09375 to 0.09375
- slot_tile: int32 [2048], replicated, may hold values from 0 to 2047, as said below
Outputs:
- hidden: bfloat16 [8192, 8192], P('dp', 'tp')
- d_normed: bfloat16 [8192, 4096], P(('dp', 'tp'))
- grad_tiles: float32 [2, 2048, 128, 128], P(None, 'tp', 'dp')
Inputs may be any that keep to these rules, and one draw needn't show every extreme that they name: `slot_tile`: A permutation of 0 to 2047. Position p belongs to owner p // 128 at slot p % 128. Each owner holds 6 to 10 tiles of the tile columns t * 4 to (t + 1) * 4 - 1 of each index t of tp; in every draw some owner holds exactly 10 for some t.
All inputs are finite; a program needn't handle non-finite values.
Results may differ from a plain program's by a relative error of at most 0.018.
Values may be sent and summed in bfloat16 or wider, within the bound.
A program may use at most 128 MiB of HBM per device.

v0:
```python
import jax
import jax.numpy as jnp
from jax import lax
from jax.sharding import Mesh
from jax.sharding import PartitionSpec as P

D = 4096
FW = 8192
TILE = 128
TP = ("tp_0", "tp_1")
DP_TP = ("dp", "tp_0", "tp_1")


def joined_along(tiles, dim):
    dims = list(tiles.shape[1:])
    dims[dim] *= tiles.shape[0]
    return jnp.moveaxis(tiles, 0, dim).reshape(dims)


def all_blocks(array, axes, order):
    tiles = array
    for k in order:
        tiles = lax.all_gather(tiles, axes[k])
    done = order[::-1]
    back = [done.index(k) for k in range(len(axes))]
    tiles = tiles.transpose(*back, *range(len(axes), tiles.ndim))
    return tiles.reshape(-1, *array.shape)


def whole_of(array, axes, order, dim):
    return joined_along(all_blocks(array, axes, order), dim)


def own_block(tiles, axes, order):
    inside = tiles.shape[1:]
    tiles = tiles.reshape(*(lax.axis_size(a) for a in axes), *inside)
    tiles = jnp.moveaxis(tiles, order, range(len(axes))).reshape(-1, *inside)
    for k in order:
        tiles = lax.psum_scatter(tiles, axes[k], scatter_dimension=0, tiled=True)
    return tiles[0]


def cut_along(array, dim, count):
    before, after = (array.shape[:dim], array.shape[dim + 1 :])
    return jnp.moveaxis(array.reshape(*before, count, -1, *after), dim, 0)


def sum_by_axis(array, axes, order, dim):
    count = lax.axis_size(axes)
    return own_block(cut_along(array, dim, count), axes, order)


def build_lists(slot_tile, groups, owned_count, tile_cols, cols_dev, list_len):
    owned_tiles = slot_tile.reshape(groups, owned_count)
    target = owned_tiles % tile_cols // cols_dev
    matches = (target[:, :, None] == jnp.arange(groups, dtype=jnp.int32)[None, None, :]).astype(
        jnp.int32
    )
    running = jnp.cumsum(matches, axis=1) - 1
    rank_of = jnp.sum(running * matches, axis=2)
    owner_ix = jnp.broadcast_to(jnp.arange(groups, dtype=jnp.int32)[:, None], (groups, owned_count))
    slot_ix = jnp.broadcast_to(
        jnp.arange(owned_count, dtype=jnp.int32)[None, :], (groups, owned_count)
    )
    table = jnp.full((groups, groups, list_len), -1, jnp.int32)
    return table.at[owner_ix, target, rank_of].set(slot_ix, mode="drop")


def incoming_places(in_lists, slot_tile, consumer, tile_cols, cols_dev, owned_count):
    groups = in_lists.shape[0]
    present = in_lists >= 0
    position = jnp.arange(groups, dtype=jnp.int32)[:, None] * owned_count + jnp.maximum(in_lists, 0)
    tile_id = slot_tile[position]
    tile_row = tile_id // tile_cols
    tile_col = tile_id % tile_cols - consumer * cols_dev
    local_idx = tile_row * cols_dev + tile_col
    return (jnp.where(present, local_idx, owned_count), present)


def pick_tiles(source, indices, present):
    limit = source.shape[1] - 1
    picked = source[:, jnp.minimum(indices, limit)]
    mask = present.reshape((1,) + present.shape + (1,) * (source.ndim - 2))
    return jnp.where(mask, picked, jnp.zeros((), source.dtype))


def place_tiles(arrived, places, owned_count):
    flat = arrived.reshape((arrived.shape[0], -1) + arrived.shape[3:])
    empty = jnp.zeros((arrived.shape[0], owned_count) + arrived.shape[3:], arrived.dtype)
    return empty.at[:, places.reshape(-1)].set(flat, mode="drop")


def local(normed, cotangent, weight_tiles, slot_tile):
    tp_size = lax.axis_size(TP)
    consumer = lax.axis_index(TP)
    owned_count = weight_tiles.shape[1]
    tile_size = weight_tiles.shape[2]
    tile_rows = D // TILE
    tile_cols = FW // TILE
    cols_dev = tile_cols // tp_size
    base_count = owned_count // tp_size
    list_len = base_count + base_count // 4
    send_lists = build_lists(slot_tile, tp_size, owned_count, tile_cols, cols_dev, list_len)
    my_lists = lax.dynamic_index_in_dim(send_lists, consumer, 0, keepdims=False)
    out_present = my_lists >= 0
    out_places = jnp.where(out_present, my_lists, owned_count)
    in_lists = lax.dynamic_index_in_dim(send_lists, consumer, 1, keepdims=False)
    in_places, in_present = incoming_places(
        in_lists, slot_tile, consumer, tile_cols, cols_dev, owned_count
    )
    slab_rows = tile_size // lax.axis_size("dp")
    slab_start = lax.axis_index("dp") * slab_rows
    own_rows = lax.dynamic_slice_in_dim(weight_tiles, slab_start, slab_rows, 2)
    outgoing = pick_tiles(own_rows, my_lists, out_present)
    arrived = lax.all_to_all(outgoing, TP, split_axis=1, concat_axis=1, tiled=True)
    partial_tiles = place_tiles(arrived, in_places, owned_count)
    weight_block = lax.all_gather(partial_tiles, "dp", axis=2, tiled=True)
    weight_block = weight_block.reshape(2, tile_rows, cols_dev, tile_size, tile_size)
    gathered = whole_of(normed, TP, (0, 1), 0)
    group_rows = gathered.shape[0]
    tiled_in = gathered.reshape(group_rows, tile_rows, tile_size)
    both_proj = jnp.einsum(
        "nri,mrcij->nmcj", tiled_in, weight_block, preferred_element_type=jnp.float32
    )
    gate_proj = both_proj[:, 0].reshape(group_rows, -1)
    up_proj = both_proj[:, 1].reshape(group_rows, -1)
    sigmoid_gate = jax.nn.sigmoid(gate_proj)
    act_gate = gate_proj * sigmoid_gate
    hidden = (act_gate * up_proj).astype(jnp.bfloat16)
    cot_full = cotangent.astype(jnp.float32)
    grad_gate = (
        cot_full * up_proj * (sigmoid_gate * (1.0 + gate_proj * (1.0 - sigmoid_gate)))
    ).astype(jnp.bfloat16)
    grad_up = (cot_full * act_gate).astype(jnp.bfloat16)
    grads_in = jnp.stack([grad_gate, grad_up], 1).reshape(group_rows, 2, cols_dev, tile_size)
    term = jnp.einsum("nmcj,mrcij->nri", grads_in, weight_block, preferred_element_type=jnp.float32)
    d_normed = (
        sum_by_axis(
            term.reshape(normed.shape[0] * lax.axis_size(TP), -1).astype(jnp.bfloat16),
            TP,
            (1, 0),
            0,
        )
        .astype(jnp.float32)
        .astype(jnp.bfloat16)
    )
    partial_value = jnp.einsum(
        "nri,nmcj->mrcij", tiled_in, grads_in, preferred_element_type=jnp.float32
    ).astype(jnp.bfloat16)
    partial_value = partial_value.reshape(2, owned_count, tile_size, tile_size)
    summed = lax.psum_scatter(partial_value, "dp", scatter_dimension=2, tiled=True).astype(
        jnp.float32
    )
    outgoing_grads = pick_tiles(summed, in_places, in_present)
    returned = lax.all_to_all(
        outgoing_grads.astype(jnp.bfloat16), TP, split_axis=1, concat_axis=1, tiled=True
    ).astype(outgoing_grads.dtype)
    result = place_tiles(returned, out_places, owned_count)
    return (hidden, d_normed, result)


def solution(mesh):
    finer = Mesh(mesh.devices.reshape(4, 4, mesh.shape["dp"]), ("tp_0", "tp_1", "dp"))
    placed = (P(DP_TP, None), P("dp", TP), P(None, TP, None, None), P())
    return jax.shard_map(
        local,
        mesh=finer,
        in_specs=placed,
        out_specs=(P("dp", TP), P(DP_TP, None), P(None, TP, "dp", None)),
        check_vma=False,
    )
```

profile of v0, /device:TPU:64, one launch (start us, length us, event | category | flops | bytes accessed | tf_op | source)
XLA Modules:
  0.0 496.8 jit_solution(926852536485832651)
XLA Ops:
  7.2 0.7 all-gather.8.cloned.1.call-update
  8.0 36.1 %all-gather.8.cloned.1.call-done = bf16[128,4096]{1,0:T(8,128)(2,1)} async-done(((bf16[32,4096]{1,0:T(8,128)(2,1)}), bf16[128,4096]{1,0:T(8,128)(2,1)}) %all-gather.8.cloned.1.call-update) | async-done | bytes 1048592 | tf_op jit(solution)/shard_map/all_gather | solution.py:23
  44.0 0.7 add_select_fusion
  44.8 0.1 copy.92
  44.9 2.8 select_reduce_fusion
  47.7 0.7 compare_select_fusion.3
  48.5 0.7 multiply_reduce_fusion
  49.2 0.7 and_reduce_fusion
  49.9 8.1 %scatter_custom_fusion.2 = s32[2560]{0:T(1024)S(1)} fusion(s32[2048]{0:T(1024)S(1)} %select_bitcast_fusion.1, s32[2048]{0:T(1024)S(1)} %iota_bitcast_fusion, s32[]{:T(128)} %constant.88.clone.1), kind=kCustom, calls=%fused_computation.81 | custom fusion | bytes 10244
  58.0 0.1 reshape.536
  58.1 0.1 copy.97
  58.2 0.1 reshape.550
  58.3 0.1 copy.96
  58.4 1.1 constant_dynamic-slice_fusion
  59.6 0.8 gather_fusion.1
  60.4 1.1 select_bitcast_fusion
  61.5 6.7 %all-to-all-start = ((bf16[2,16,10,8,128]{4,3,0,2,1:T(8,128)(2,1)}), bf16[2,16,10,8,128]{4,3,0,2,1:T(8,128)(2,1)S(1)}, u32[]{:S(2)}, u32[]{:S(2)}) async-start(bf16[2,16,10,8,128]{4,3,0,2,1:T(8,128)(2,1)} %select_bitcast_fusion), calls=%async_computation | async-start | bytes 1310720 | tf_op jit(solution)/shard_map/all_to_all | solution.py:115
  68.2 0.1 compare_bitcast_fusion
  68.3 0.2 copy.94
  68.5 0.1 ge.52
  68.6 0.3 bitcast_reduce_fusion
  68.9 0.1 copy.95
  69.0 0.1 reshape.542
  69.1 1.4 gather_fusion
  70.6 14.5 %all-to-all-done = bf16[2,16,10,8,128]{4,3,0,2,1:T(8,128)(2,1)S(1)} async-done(((bf16[2,16,10,8,128]{4,3,0,2,1:T(8,128)(2,1)}), bf16[2,16,10,8,128]{4,3,0,2,1:T(8,128)(2,1)S(1)}, u32[]{:S(2)}, u32[]{:S(2)}) %all-to-all-start) | async-done | bytes 655392 | tf_op jit(solution)/shard_map/all_to_all | solution.py:115
  85.2 6.9 %scatter_fusion = bf16[2,128,8,128]{3,2,1,0:T(8,128)(2,1)S(1)} fusion(bf16[2,128,8,128]{3,2,1,0:T(8,128)(2,1)S(1)} %broadcast_in_dim.63, s32[160]{0:T(256)S(1)} %bitcast.163, bf16[160,2,8,128]{3,2,1,0:T(8,128)(2,1)S(1)} %bitcast.151), kind=kCustom, calls=%fused_computation.3 | custom fusion | bytes 1966720 | tf_op jit(solution)/shard_map/scatter | solution.py:90
  92.0 0.8 copy-done.1
  92.9 0.2 reduce-scatter.6.cloned.1.call-start
  93.1 0.2 copy.101
  93.3 10.9 %all-gather.10.cloned.1.call-done = bf16[16,32,4096]{2,1,0:T(8,128)(2,1)} async-done(((bf16[4,32,4096]{2,1,0:T(8,128)(2,1)}), bf16[16,32,4096]{2,1,0:T(8,128)(2,1)}) %all-gather.10.cloned.1.call-update) | async-done | bytes 4194320 | tf_op jit(solution)/shard_map/all_gather | solution.py:23
  104.2 2.5 copy.98
  106.6 3.2 copy.134
  109.9 108.0 %all-gather.6.cloned.1.call-done = bf16[2,128,128,128]{3,2,1,0:T(8,128)(2,1)} async-done(((bf16[2,128,8,128]{3,2,1,0:T(8,128)(2,1)}), bf16[2,128,128,128]{3,2,1,0:T(8,128)(2,1)}) %all-gather.6.cloned.1.call-update) | async-done | bytes 8388624 | tf_op jit(solution)/shard_map/all_gather | solution.py:117
  217.9 10.5 %fusion.4 = f32[512,2,4,128]{0,3,2,1:T(8,128)S(1)} fusion(bf16[2,32,4,128,128]{4,3,2,1,0:T(8,128)(2,1)} %bitcast.144, bf16[512,32,128,1,1]{2,1,0,4,3:T(8,128)(2,1)} %bitcast.148), kind=kOutput, calls=%fused_computation.13 | convolution fusion | flops 4294967296 | bytes 14680064 | tf_op jit(solution)/shard_map/nri,mrcij->nmcj/dot_general | solution.py:122
  228.4 0.2 fusion.37
  228.6 10.3 %copy.104 = bf16[32,128,4,128,2]{3,1,0,4,2:T(8,128)(2,1)} copy(bf16[32,128,4,128,2]{3,1,2,0,4:T(8,128)(2,1)} %bitcast.145) | data formatting | bytes 16777216 | tf_op jit(solution)/shard_map/nmcj,mrcij->nri/dot_general | solution.py:136
  238.9 0.7 fusion.8
  239.6 0.3 copy.103
  239.9 0.3 copy.102
  240.2 8.2 %bitcast_convert_fusion = bf16[512,4096]{1,0:T(8,128)(2,1)S(1)} fusion(bf16[4096,4,128,2]{2,0,3,1:T(8,128)(2,1)} %bitcast.146, bf16[512,1,4,128]{3,0,1,2:T(8,128)(2,1)S(1)} %copy.103, bf16[512,1,4,128]{3,0,1,2:T(8,128)(2,1)S(1)} %copy.102), kind=kOutput, calls=%fused_computation.7 | convolution fusion | flops 4297588736 | bytes 13631488 | tf_op jit(solution)/shard_map/nmcj,mrcij->nri/dot_general | solution.py:136
  248.3 2.5 copy.105
  250.9 9.6 %convert_bitcast_fusion = bf16[2,32,4,128,128]{3,4,1,2,0:T(8,128)(2,1)} fusion(bf16[512,32,128,1,1]{2,1,0,4,3:T(8,128)(2,1)} %bitcast.149, bf16[512,1,4,128]{3,0,1,2:T(8,128)(2,1)S(1)} %copy.103, bf16[512,1,4,128]{3,0,1,2:T(8,128)(2,1)S(1)} %copy.102), kind=kOutput, calls=%fused_computation.8 | convolution fusion | flops 4299685888 | bytes 13631488 | tf_op jit(solution)/shard_map/nri,nmcj->mrcij/dot_general | solution.py:147
  260.5 12.1 %copy.110 = bf16[2,32,4,128,128]{4,3,2,1,0:T(8,128)(2,1)} copy(bf16[2,32,4,128,128]{3,4,1,2,0:T(8,128)(2,1)} %convert_bitcast_fusion) | data formatting | bytes 16777216 | tf_op jit(solution)/shard_map/convert_element_type | solution.py:149
  272.6 12.1 %copy.132 = bf16[2,128,128,128]{3,1,0,2:T(8,128)(2,1)} copy(bf16[2,128,128,128]{3,2,1,0:T(8,128)(2,1)} %bitcast.140) | data formatting | bytes 16777216
  284.7 13.9 %copy.150 = bf16[16,8,256,128]{3,1,2,0:T(8,128)(2,1)} copy(bf16[16,8,256,128]{3,2,1,0:T(8,128)(2,1)} %bitcast.141) | data formatting | bytes 16777216
  298.7 0.1 gather.16
  298.8 0.1 copy.116
  298.9 0.1 copy.112
  298.9 0.2 reduce-scatter.8.cloned.1.call-update
  299.3 0.1 copy.117
  299.3 0.1 reshape.558
  299.5 141.2 %reduce-scatter.10.cloned.1.call-done = bf16[8,32768]{1,0:T(8,128)(2,1)} async-done(((bf16[128,32768]{1,0:T(8,128)(2,1)}), bf16[8,32768]{1,0:T(8,128)(2,1)}) %reduce-scatter.10.cloned.1.call-update) | async-done | bytes 524304
  440.7 1.1 copy.136
  441.8 0.3 copy.149
  442.1 0.8 gather_fusion.2
  442.9 1.1 fusion.20
  444.0 6.8 %all-to-all-start.1 = ((bf16[2,16,10,8,128]{4,3,0,2,1:T(8,128)(2,1)}), bf16[2,16,10,8,128]{4,3,0,2,1:T(8,128)(2,1)S(1)}, u32[]{:S(2)}, u32[]{:S(2)}) async-start(bf16[2,16,10,8,128]{4,3,0,2,1:T(8,128)(2,1)} %fusion.20), calls=%async_computation.3 | async-start | bytes 1310720 | tf_op jit(solution)/shard_map/all_to_all | solution.py:155
  450.8 0.1 copy.106
  450.9 0.1 squeeze.10
  451.0 1.0 copy.118
  452.0 30.0 %all-to-all-done.1 = bf16[2,16,10,8,128]{4,3,0,2,1:T(8,128)(2,1)S(1)} async-done(((bf16[2,16,10,8,128]{4,3,0,2,1:T(8,128)(2,1)}), bf16[2,16,10,8,128]{4,3,0,2,1:T(8,128)(2,1)S(1)}, u32[]{:S(2)}, u32[]{:S(2)}) %all-to-all-start.1) | async-done | bytes 655392 | tf_op jit(solution)/shard_map/all_to_all | solution.py:155
  482.0 0.1 convert_bitcast_fusion.1
  482.2 6.8 %scatter_fusion.1 = f32[2,128,8,128]{3,2,1,0:T(8,128)S(1)} fusion(f32[2,128,8,128]{3,2,1,0:T(8,128)S(1)} %broadcast_in_dim.71, s32[160]{0:T(256)S(1)} %bitcast.164, f32[160,2,8,128]{3,2,1,0:T(8,128)S(1)} %convert_bitcast_fusion.1), kind=kCustom, calls=%fused_computation.4 | custom fusion | bytes 3932800 | tf_op jit(solution)/shard_map/scatter | solution.py:90
  489.1 0.9 copy-done.2
  (33 shorter events, 0.7 us)
Async XLA Ops:
  7.2 62.0 %copy-start = (s32[2048]{0:T(1024)S(1)}, s32[2048]{0:T(1024)}, u32[]{:S(2)}) copy-start(s32[2048]{0:T(1024)} %param.7) | copy-start | bytes 24580
  7.2 36.8 %all-gather.8.cloned.1.call-start = ((), (), s32[]{:S(2)}) async-start(), calls=%async_computation.8 | async-start | bytes 1310720 | tf_op jit(solution)/shard_map/all_gather | solution.py:23
  7.9 96.3 %all-gather.10.cloned.1.call-start = ((), (), s32[]{:S(2)}) async-start(), calls=%async_computation.9 | async-start | bytes 5242880 | tf_op jit(solution)/shard_map/all_gather | solution.py:23
  61.5 23.6 %all-to-all-start = ((bf16[2,16,10,8,128]{4,3,0,2,1:T(8,128)(2,1)}), bf16[2,16,10,8,128]{4,3,0,2,1:T(8,128)(2,1)S(1)}, u32[]{:S(2)}, u32[]{:S(2)}) async-start(bf16[2,16,10,8,128]{4,3,0,2,1:T(8,128)(2,1)} %select_bitcast_fusion), calls=%async_computation | async-start | bytes 1310720 | tf_op jit(solution)/shard_map/all_to_all | solution.py:115
  68.1 149.8 %all-gather.6.cloned.1.call-start = ((), (), s32[]{:S(2)}) async-start(), calls=%async_computation.5 | async-start | bytes 8912896 | tf_op jit(solution)/shard_map/all_gather | solution.py:117
  69.1 23.9 %copy-start.3 = (bf16[512,512]{1,0:T(8,128)(2,1)S(1)}, bf16[512,512]{1,0:T(8,128)(2,1)}, u32[]{:S(2)}) copy-start(bf16[512,512]{1,0:T(8,128)(2,1)} %param.5) | copy-start | bytes 1572868
  92.0 0.8 copy-start.1
  92.9 206.1 %reduce-scatter.6.cloned.1.call-start = ((), (), s32[]{:S(2)}) async-start(), calls=%async_computation.6 | async-start | bytes 5242880 | tf_op jit(solution)/shard_map/reduce_scatter | solution.py:39
  250.8 189.8 %reduce-scatter.10.cloned.1.call-start = ((), (), s32[]{:S(2)}) async-start(), calls=%async_computation.10 | async-start | bytes 8912896
  298.6 190.4 %reduce-scatter.8.cloned.1.call-start = ((), (), s32[]{:S(2)}) async-start(), calls=%async_computation.7 | async-start | bytes 1310720 | tf_op jit(solution)/shard_map/reduce_scatter | solution.py:39
  444.0 38.0 %all-to-all-start.1 = ((bf16[2,16,10,8,128]{4,3,0,2,1:T(8,128)(2,1)}), bf16[2,16,10,8,128]{4,3,0,2,1:T(8,128)(2,1)S(1)}, u32[]{:S(2)}, u32[]{:S(2)}) async-start(bf16[2,16,10,8,128]{4,3,0,2,1:T(8,128)(2,1)} %fusion.20), calls=%async_computation.3 | async-start | bytes 1310720 | tf_op jit(solution)/shard_map/all_to_all | solution.py:155
  489.0 1.0 copy-start.2
Sparse Core Ops, SparseCore 0:
  9.8 34.1 all-gather.7
  45.8 58.3 all-gather.9
  107.3 110.5 all-gather.5
  250.9 47.2 reduce-scatter.5
  302.7 137.9 reduce-scatter.9
  443.6 38.5 reduce-scatter.7
where the time goes:
time: 498 us; the launch traced here: 497 us
  waiting for transfers between devices  342 us (69%)
  local copies, waits for them, and re-layouts  89.4 us (18%)
  matrix products  28.3 us (6%)
  between operations  14.4 us (3%)
  starting transfers between devices  13.9 us (3%)
  other arithmetic  9.23 us (2%)
    unnamed x7, waiting for transfers between devices  142 us
    all_gather x1, waiting for transfers between devices, local(): weight_block = lax.all_gather(partial_tiles, 'dp', axis=2, tiled=True)  108 us
    all_gather x2, waiting for transfers between devices, all_blocks(): tiles = lax.all_gather(tiles, axes[k])  46.9 us
    unnamed x17, local copies, waits for them, and re-layouts  41.8 us
    all_to_all x1, waiting for transfers between devices, local(): lax.all_to_all(outgoing_grads.astype(jnp.bfloat16), TP, split_axis=1, con...  30 us
    all_to_all x1, waiting for transfers between devices, local(): lax.all_to_all(outgoing, TP, split_axis=1, concat_axis=1, tiled=True)  14.5 us
    scatter x2, local copies, waits for them, and re-layouts, place_tiles(): return empty.at[:, places.reshape(-1)].set(flat, mode='drop')  13.7 us
    convert_element_type x1, local copies, waits for them, and re-layouts, local(): partial_value = jnp.einsum('nri,nmcj->mrcij', tiled_in, grads_in, preferr...  12.1 us
  transfers between devices with their start and end apart: 8, of which 6 were waited for; matrix products, arithmetic and copies ran while one was open for 19% of the time, Pallas kernels for 0%

commit v1 on v0

--- a/solution.py
+++ b/solution.py
@@ -152,8 +152,14 @@
         jnp.float32
     )
     outgoing_grads = pick_tiles(summed, in_places, in_present)
-    returned = lax.all_to_all(
-        outgoing_grads.astype(jnp.bfloat16), TP, split_axis=1, concat_axis=1, tiled=True
+    returned = jnp.concatenate(
+        lax.all_to_all(
+            jnp.stack(jnp.split(outgoing_grads.astype(jnp.bfloat16), lax.axis_size(TP), axis=1)),
+            TP,
+            0,
+            0,
+        ),
+        axis=1,
     ).astype(outgoing_grads.dtype)
     result = place_tiles(returned, out_places, owned_count)
     return (hidden, d_normed, result)

time: 498 us -> 503 us (1.010)
  local copies, waits for them, and re-layouts: 89.4 us -> 99.3 us
    unnamed x17 -> x32, local copies, waits for them, and re-layouts: 41.8 us -> 51.1 us
  transfers between devices with their start and end apart: 8 -> 8, of which waited for: 6 -> 6; matrix products, arithmetic and copies ran while one was open for 19% -> 20% of each run, Pallas kernels for 0% -> 0%
where the time goes in v1:
time: 503 us; the launch traced here: 502 us
  waiting for transfers between devices  337 us (67%)
  local copies, waits for them, and re-layouts  99.3 us (20%)
  matrix products  28.3 us (6%)
  between operations  14.5 us (3%)
  starting transfers between devices  13.9 us (3%)
  other arithmetic  8.39 us (2%)
    unnamed x7, waiting for transfers between devices  142 us
    all_gather x1, waiting for transfers between devices, local(): weight_block = lax.all_gather(partial_tiles, 'dp', axis=2, tiled=True)  108 us
    unnamed x32, local copies, waits for them, and re-layouts  51.1 us
    all_gather x2, waiting for transfers between devices, all_blocks(): tiles = lax.all_gather(tiles, axes[k])  46.9 us
    all_to_all x1, waiting for transfers between devices, local(): lax.all_to_all(jnp.stack(jnp.split(outgoing_grads.astype(jnp.bfloat16), l...  25.6 us
    all_to_all x1, waiting for transfers between devices, local(): lax.all_to_all(outgoing, TP, split_axis=1, concat_axis=1, tiled=True)  14.5 us
    scatter x2, local copies, waits for them, and re-layouts, place_tiles(): return empty.at[:, places.reshape(-1)].set(flat, mode='drop')  13.7 us
    convert_element_type x1, local copies, waits for them, and re-layouts, local(): partial_value = jnp.einsum('nri,nmcj->mrcij', tiled_in, grads_in, preferr...  12.1 us
  transfers between devices with their start and end apart: 8, of which 6 were waited for; matrix products, arithmetic and copies ran while one was open for 20% of the time, Pallas kernels for 0%

profile of v1, /device:TPU:64, one launch (start us, length us, event | category | flops | bytes accessed | tf_op | source)
XLA Modules:
  0.0 501.5 jit_solution(18203628336199092500)
XLA Ops:
  7.2 0.7 all-gather.8.cloned.1.call-update
  8.0 36.1 %all-gather.8.cloned.1.call-done = bf16[128,4096]{1,0:T(8,128)(2,1)} async-done(((bf16[32,4096]{1,0:T(8,128)(2,1)}), bf16[128,4096]{1,0:T(8,128)(2,1)}) %all-gather.8.cloned.1.call-update) | async-done | bytes 1048592 | tf_op jit(solution)/shard_map/all_gather | solution.py:23
  44.0 0.7 add_select_fusion
  44.9 2.8 select_reduce_fusion
  47.7 0.7 compare_select_fusion.3
  48.5 0.7 multiply_reduce_fusion
  49.2 0.7 and_reduce_fusion
  49.9 8.1 %scatter_custom_fusion.2 = s32[2560]{0:T(1024)S(1)} fusion(s32[2048]{0:T(1024)S(1)} %select_bitcast_fusion.1, s32[2048]{0:T(1024)S(1)} %iota_bitcast_fusion, s32[]{:T(128)} %constant.88.clone.1), kind=kCustom, calls=%fused_computation.112 | custom fusion | bytes 10244
  58.4 1.1 constant_dynamic-slice_fusion
  59.6 0.8 gather_fusion.1
  60.4 1.1 select_bitcast_fusion
  61.5 6.7 %all-to-all-start = ((bf16[2,16,10,8,128]{4,3,0,2,1:T(8,128)(2,1)}), bf16[2,16,10,8,128]{4,3,0,2,1:T(8,128)(2,1)S(1)}, u32[]{:S(2)}, u32[]{:S(2)}) async-start(bf16[2,16,10,8,128]{4,3,0,2,1:T(8,128)(2,1)} %select_bitcast_fusion), calls=%async_computation | async-start | bytes 1310720 | tf_op jit(solution)/shard_map/all_to_all | solution.py:115
  68.3 0.2 copy.109
  68.6 0.3 bitcast_reduce_fusion
  69.1 1.4 gather_fusion
  70.6 14.5 %all-to-all-done = bf16[2,16,10,8,128]{4,3,0,2,1:T(8,128)(2,1)S(1)} async-done(((bf16[2,16,10,8,128]{4,3,0,2,1:T(8,128)(2,1)}), bf16[2,16,10,8,128]{4,3,0,2,1:T(8,128)(2,1)S(1)}, u32[]{:S(2)}, u32[]{:S(2)}) %all-to-all-start) | async-done | bytes 655392 | tf_op jit(solution)/shard_map/all_to_all | solution.py:115
  85.2 6.9 %scatter_fusion = bf16[2,128,8,128]{3,2,1,0:T(8,128)(2,1)S(1)} fusion(bf16[2,128,8,128]{3,2,1,0:T(8,128)(2,1)S(1)} %broadcast_in_dim.63, s32[160]{0:T(256)S(1)} %bitcast.228, bf16[160,2,8,128]{3,2,1,0:T(8,128)(2,1)S(1)} %bitcast.216), kind=kCustom, calls=%fused_computation.3 | custom fusion | bytes 1966720 | tf_op jit(solution)/shard_map/scatter | solution.py:90
  92.0 0.8 copy-done.1
  92.9 0.2 reduce-scatter.6.cloned.1.call-start
  93.1 0.2 copy.116
  93.3 10.9 %all-gather.10.cloned.1.call-done = bf16[16,32,4096]{2,1,0:T(8,128)(2,1)} async-done(((bf16[4,32,4096]{2,1,0:T(8,128)(2,1)}), bf16[16,32,4096]{2,1,0:T(8,128)(2,1)}) %all-gather.10.cloned.1.call-update) | async-done | bytes 4194320 | tf_op jit(solution)/shard_map/all_gather | solution.py:23
  104.2 2.5 copy.113
  106.6 3.2 copy.149
  109.9 108.0 %all-gather.6.cloned.1.call-done = bf16[2,128,128,128]{3,2,1,0:T(8,128)(2,1)} async-done(((bf16[2,128,8,128]{3,2,1,0:T(8,128)(2,1)}), bf16[2,128,128,128]{3,2,1,0:T(8,128)(2,1)}) %all-gather.6.cloned.1.call-update) | async-done | bytes 8388624 | tf_op jit(solution)/shard_map/all_gather | solution.py:117
  217.9 10.5 %fusion.4 = f32[512,2,4,128]{0,3,2,1:T(8,128)S(1)} fusion(bf16[2,32,4,128,128]{4,3,2,1,0:T(8,128)(2,1)} %bitcast.208, bf16[512,32,128,1,1]{2,1,0,4,3:T(8,128)(2,1)} %bitcast.213), kind=kOutput, calls=%fused_computation.13 | convolution fusion | flops 4294967296 | bytes 14680064 | tf_op jit(solution)/shard_map/nri,mrcij->nmcj/dot_general | solution.py:122
  228.4 0.2 fusion.53
  228.6 10.3 %copy.119 = bf16[32,128,4,128,2]{3,1,0,4,2:T(8,128)(2,1)} copy(bf16[32,128,4,128,2]{3,1,2,0,4:T(8,128)(2,1)} %bitcast.209) | data formatting | bytes 16777216 | tf_op jit(solution)/shard_map/nmcj,mrcij->nri/dot_general | solution.py:136
  238.9 0.7 fusion.8
  239.6 0.3 copy.118
  239.9 0.3 copy.117
  240.2 8.2 %bitcast_convert_fusion = bf16[512,4096]{1,0:T(8,128)(2,1)S(1)} fusion(bf16[4096,4,128,2]{2,0,3,1:T(8,128)(2,1)} %bitcast.210, bf16[512,1,4,128]{3,0,1,2:T(8,128)(2,1)S(1)} %copy.118, bf16[512,1,4,128]{3,0,1,2:T(8,128)(2,1)S(1)} %copy.117), kind=kOutput, calls=%fused_computation.7 | convolution fusion | flops 4297588736 | bytes 13631488 | tf_op jit(solution)/shard_map/nmcj,mrcij->nri/dot_general | solution.py:136
  248.3 2.5 copy.120
  250.9 9.6 %convert_bitcast_fusion = bf16[2,32,4,128,128]{3,4,1,2,0:T(8,128)(2,1)} fusion(bf16[512,32,128,1,1]{2,1,0,4,3:T(8,128)(2,1)} %bitcast.214, bf16[512,1,4,128]{3,0,1,2:T(8,128)(2,1)S(1)} %copy.118, bf16[512,1,4,128]{3,0,1,2:T(8,128)(2,1)S(1)} %copy.117), kind=kOutput, calls=%fused_computation.8 | convolution fusion | flops 4299685888 | bytes 13631488 | tf_op jit(solution)/shard_map/nri,nmcj->mrcij/dot_general | solution.py:147
  260.5 12.1 %copy.125 = bf16[2,32,4,128,128]{4,3,2,1,0:T(8,128)(2,1)} copy(bf16[2,32,4,128,128]{3,4,1,2,0:T(8,128)(2,1)} %convert_bitcast_fusion) | data formatting | bytes 16777216 | tf_op jit(solution)/shard_map/convert_element_type | solution.py:149
  272.6 12.1 %copy.147 = bf16[2,128,128,128]{3,1,0,2:T(8,128)(2,1)} copy(bf16[2,128,128,128]{3,2,1,0:T(8,128)(2,1)} %bitcast.204) | data formatting | bytes 16777216
  284.7 13.9 %copy.165 = bf16[16,8,256,128]{3,1,2,0:T(8,128)(2,1)} copy(bf16[16,8,256,128]{3,2,1,0:T(8,128)(2,1)} %bitcast.205) | data formatting | bytes 16777216
  298.8 0.1 copy.131
  299.3 141.4 %reduce-scatter.10.cloned.1.call-done = bf16[8,32768]{1,0:T(8,128)(2,1)} async-done(((bf16[128,32768]{1,0:T(8,128)(2,1)}), bf16[8,32768]{1,0:T(8,128)(2,1)}) %reduce-scatter.10.cloned.1.call-update) | async-done | bytes 524304
  440.7 1.1 copy.151
  441.8 0.3 copy.164
  442.1 0.8 gather_fusion.2
  442.9 0.2 fusion.20
  443.2 0.6 fusion.37
  443.8 0.6 fusion.36
  444.4 0.6 fusion.35
  445.0 0.6 fusion.34
  445.7 0.6 fusion.33
  446.3 0.6 fusion.32
  446.9 0.6 fusion.31
  447.5 0.6 fusion.30
  448.1 0.6 fusion.29
  448.8 0.6 fusion.28
  449.4 0.6 fusion.27
  450.0 0.6 fusion.26
  450.6 0.6 fusion.25
  451.2 0.6 fusion.24
  451.9 0.6 fusion.23
  452.5 0.6 fusion.22
  453.1 6.8 %all-to-all-start.1 = ((bf16[16,2,1,10,8,128]{5,4,1,3,2,0:T(8,128)(2,1)}), bf16[16,2,1,10,8,128]{5,4,1,3,2,0:T(8,128)(2,1)S(1)}, u32[]{:S(2)}, u32[]{:S(2)}) async-start(bf16[16,2,1,10,8,128]{5,4,1,3,2,0:T(8,128)(2,1)} %fusion.22), calls=%async_computation.3 | async-start | bytes 1310720 | tf_op jit(solution)/shard_map/all_to_all | solution.py:156
  460.1 1.0 copy.133
  461.1 25.6 %all-to-all-done.1 = bf16[16,2,1,10,8,128]{5,4,1,3,2,0:T(8,128)(2,1)S(1)} async-done(((bf16[16,2,1,10,8,128]{5,4,1,3,2,0:T(8,128)(2,1)}), bf16[16,2,1,10,8,128]{5,4,1,3,2,0:T(8,128)(2,1)S(1)}, u32[]{:S(2)}, u32[]{:S(2)}) %all-to-all-start.1) | async-done | bytes 655392 | tf_op jit(solution)/shard_map/all_to_all | solution.py:156
  486.7 0.1 convert_element_type.56
  486.9 6.8 %scatter_fusion.1 = f32[2,128,8,128]{3,2,1,0:T(8,128)S(1)} fusion(f32[2,128,8,128]{3,2,1,0:T(8,128)S(1)} %broadcast_in_dim.71, s32[160]{0:T(256)S(1)} %bitcast.229, f32[160,2,8,128]{3,2,1,0:T(8,128)S(1)} %bitcast.211), kind=kCustom, calls=%fused_computation.4 | custom fusion | bytes 3932800 | tf_op jit(solution)/shard_map/scatter | solution.py:90
  493.8 0.9 copy-done.2
  (49 shorter events, 2.0 us)
Async XLA Ops:
  7.2 62.0 %copy-start = (s32[2048]{0:T(1024)S(1)}, s32[2048]{0:T(1024)}, u32[]{:S(2)}) copy-start(s32[2048]{0:T(1024)} %param.7) | copy-start | bytes 24580
  7.2 36.8 %all-gather.8.cloned.1.call-start = ((), (), s32[]{:S(2)}) async-start(), calls=%async_computation.8 | async-start | bytes 1310720 | tf_op jit(solution)/shard_map/all_gather | solution.py:23
  7.9 96.3 %all-gather.10.cloned.1.call-start = ((), (), s32[]{:S(2)}) async-start(), calls=%async_computation.9 | async-start | bytes 5242880 | tf_op jit(solution)/shard_map/all_gather | solution.py:23
  61.5 23.6 %all-to-all-start = ((bf16[2,16,10,8,128]{4,3,0,2,1:T(8,128)(2,1)}), bf16[2,16,10,8,128]{4,3,0,2,1:T(8,128)(2,1)S(1)}, u32[]{:S(2)}, u32[]{:S(2)}) async-start(bf16[2,16,10,8,128]{4,3,0,2,1:T(8,128)(2,1)} %select_bitcast_fusion), calls=%async_computation | async-start | bytes 1310720 | tf_op jit(solution)/shard_map/all_to_all | solution.py:115
  68.1 149.8 %all-gather.6.cloned.1.call-start = ((), (), s32[]{:S(2)}) async-start(), calls=%async_computation.5 | async-start | bytes 8912896 | tf_op jit(solution)/shard_map/all_gather | solution.py:117
  69.1 23.9 %copy-start.3 = (bf16[512,512]{1,0:T(8,128)(2,1)S(1)}, bf16[512,512]{1,0:T(8,128)(2,1)}, u32[]{:S(2)}) copy-start(bf16[512,512]{1,0:T(8,128)(2,1)} %param.5) | copy-start | bytes 1572868
  92.0 0.8 copy-start.1
  92.9 206.4 %reduce-scatter.6.cloned.1.call-start = ((), (), s32[]{:S(2)}) async-start(), calls=%async_computation.6 | async-start | bytes 5242880 | tf_op jit(solution)/shard_map/reduce_scatter | solution.py:39
  250.8 189.8 %reduce-scatter.10.cloned.1.call-start = ((), (), s32[]{:S(2)}) async-start(), calls=%async_computation.10 | async-start | bytes 8912896
  298.6 195.1 %reduce-scatter.8.cloned.1.call-start = ((), (), s32[]{:S(2)}) async-start(), calls=%async_computation.7 | async-start | bytes 1310720 | tf_op jit(solution)/shard_map/reduce_scatter | solution.py:39
  453.1 33.6 %all-to-all-start.1 = ((bf16[16,2,1,10,8,128]{5,4,1,3,2,0:T(8,128)(2,1)}), bf16[16,2,1,10,8,128]{5,4,1,3,2,0:T(8,128)(2,1)S(1)}, u32[]{:S(2)}, u32[]{:S(2)}) async-start(bf16[16,2,1,10,8,128]{5,4,1,3,2,0:T(8,128)(2,1)} %fusion.22), calls=%async_computation.3 | async-start | bytes 1310720 | tf_op jit(solution)/shard_map/all_to_all | solution.py:156
  493.7 1.0 copy-start.2
Sparse Core Ops, SparseCore 0:
  9.8 34.1 all-gather.7
  45.8 58.3 all-gather.9
  107.3 110.5 all-gather.5
  250.9 47.2 reduce-scatter.5
  302.7 137.9 reduce-scatter.9
  443.6 39.3 reduce-scatter.7
